TPU v7x, 128 devices: a whole 4x4x4 slice. The times are simulated.
128 devices in a mesh: tp: 2 (over core), sp: 64 (over z, y, x).
Axes of the slice: x: 4, y: 4, z: 4, core: 2. Of those that a mesh axis runs over, the one named last changes fastest.
Arguments:
- x: bfloat16 [8, 4096], replicated
- seq_len: int32 [8], replicated
- ln_w: bfloat16 [4096], replicated
- w_q: bfloat16 [4096, 4096], P(None, 'tp')
- w_o: bfloat16 [4096, 4096], P('tp')
- w_gate: bfloat16 [4096, 12288], P(None, 'tp')
- w_up: bfloat16 [4096, 12288], P(None, 'tp')
- w_down: bfloat16 [12288, 4096], P('tp')
- k_cache: bfloat16 [8, 8, 32768, 128], P(None, 'tp', 'sp')
- v_cache: bfloat16 [8, 8, 32768, 128], P(None, 'tp', 'sp')
Outputs:
- output: bfloat16 [8, 4096], replicated
All inputs are finite; a program needn't handle non-finite values.
Results may differ from a plain program's by a relative error of at most 0.00725907.
Values sent between devices are 32-bit elements.
A program may use at most 1 GiB of HBM per device.

v0:
```python
import jax
import jax.numpy as jnp
from jax import lax
from jax.experimental import pallas as pl
from jax.experimental.pallas import tpu as pltpu
from jax.sharding import PartitionSpec as P

LN_EPS = 1e-5
NEG_BIG = -1e30
MESH = pl.DeviceIdType.MESH
SIDE = 4
N_SP = SIDE ** 3
N_CHIPS = 8
N_GROUP = 2 * N_CHIPS
LANES = 128
Q_CHUNKS = (1024, 1024, 1024, 512, 256, 256)
V_GROUPS = (4, 3, 1)
N_INNER = 48


def hops(d):
    return min(d, SIDE - d)


STEPS = sorted(((dz, dy, dx) for dz in range(SIDE) for dy in range(SIDE) for dx in range(SIDE) if dz or dy or dx),
               key=lambda s: -sum(hops(d) for d in s))
FINISH_ORDER = (
    0, 12, 3, 1, 4, 16, 2, 57, 54, 8, 48, 35, 6, 19, 34, 36,
    40, 7, 49, 42, 15, 56, 31, 25, 62, 37, 41, 14, 59, 28, 45, 11,
    22, 32, 47, 58, 23, 44, 20, 60, 24, 51, 17, 46, 5, 43, 38, 9,
    18, 52, 21, 53, 63, 29, 30, 26, 33, 61, 27, 10, 55, 39, 50, 13,
)
FLIPS = sorted(((fz, fy, fx) for fz in range(2) for fy in range(2) for fx in range(2) if fz or fy or fx),
               key=lambda s: -sum(s))


COMBINE_ORDER = (
    0, 32, 8, 40, 34, 10, 2, 42, 6, 38, 4, 36, 46, 9, 63, 56,
    24, 33, 43, 41, 1, 26, 37, 7, 16, 53, 5, 39, 35, 29, 11, 3,
    14, 51, 58, 52, 47, 60, 49, 44, 57, 50, 61, 45, 12, 17, 15, 27,
    19, 48, 20, 25, 55, 22, 30, 21, 31, 59, 13, 54, 23, 62, 28, 18,
)


def slot_of(sp):
    z, y, x = sp // 16, sp // 4 % 4, sp % 4
    return 32 * (z // 2) + 4 * (z % 2) + 16 * (y // 2) + 2 * (y % 2) + 8 * (x // 2) + x % 2


def kernel(seq_hbm, x_hbm, lnw_hbm, wq_hbm, wo_hbm, wg_hbm, wu_hbm, wd_hbm, k_hbm, v_hbm, out_ref,
           seq_ref, x_v, lnw_v, h_v, wq_v, k_v, v_v, wg_v, wu_v, wd_v, wo_v, q_v, s_v, p_v, stat_v, lse_v,
           att_send, att_recv, mlp_send, mlp_recv, half_send, half_recv, sum_send, sum_recv, fin,
           x_sem, wq_sem, k_sem, v_sem, w_sem, send_sem, att_rs, mlp_rs, half_rs, sum_rs, fin_rs):
    n_rows, width = x_v.shape
    n_kv, seq_block, head_dim = k_v.shape[1:]
    n_heads = q_v.shape[0] // n_rows
    inner = wg_v.shape[1]
    o_rows = wo_v.shape[0]
    per_row = n_kv // 2
    piece = width // N_CHIPS
    piece_rows = piece // LANES
    tp = lax.axis_index('tp')
    sp = lax.axis_index('sp')
    z, y, x = lax.div(sp, 16), lax.rem(lax.div(sp, 4), 4), lax.rem(sp, 4)
    zs, ys, xs = ([lax.rem(c + d, SIDE) for d in range(SIDE)] for c in (z, y, x))
    mine = (32 * lax.div(z, 2) + 4 * lax.rem(z, 2) + 16 * lax.div(y, 2) + 2 * lax.rem(y, 2)
            + 8 * lax.div(x, 2) + lax.rem(x, 2))
    row, corner = lax.div(mine, N_CHIPS), lax.rem(mine, N_CHIPS)
    at_z, at_y = [16 * c for c in zs], [4 * c for c in ys]
    flip_z, flip_y, flip_x = ([c, c + 1 - 2 * lax.rem(c, 2)] for c in (z, y, x))

    def step_to(s):
        return at_z[s[0]] + at_y[s[1]] + xs[s[2]]

    def in_order(order):
        for to in order[:-1]:
            is_me = sp == to
            yield jnp.where(is_me, order[-1], to), jnp.where(is_me, slot_of(order[-1]), slot_of(to))

    def flip_to(f):
        return 16 * flip_z[f[0]] + 4 * flip_y[f[1]] + flip_x[f[2]]

    q_starts = [sum(Q_CHUNKS[:i]) for i in range(len(Q_CHUNKS))]
    v_starts = [sum(V_GROUPS[:i]) for i in range(len(V_GROUPS))]

    def wq_copy(i):
        at = pl.ds(q_starts[i], Q_CHUNKS[i])
        return pltpu.make_async_copy(wq_hbm.at[at], wq_v.at[at], wq_sem.at[i])

    def k_copy(i):
        at = pl.ds(i * (n_rows // 2), n_rows // 2)
        return pltpu.make_async_copy(k_hbm.at[at], k_v.at[at], k_sem.at[i])

    def v_copy(i):
        at = pl.ds(v_starts[i], V_GROUPS[i])
        return pltpu.make_async_copy(v_hbm.at[at], v_v.at[at], v_sem.at[i])

    quarter = 2 * lax.div(z, 2) + lax.div(y, 2)
    shares_mlp = quarter < 3
    share = lax.rem(16 * quarter + 8 * lax.rem(z, 2) + 4 * lax.rem(y, 2) + x, N_INNER)
    inner_at = pl.multiple_of(share * inner, LANES)
    wg_copy = pltpu.make_async_copy(wg_hbm.at[:, pl.ds(inner_at, inner)], wg_v, w_sem.at[0])
    wu_copy = pltpu.make_async_copy(wu_hbm.at[:, pl.ds(inner_at, inner)], wu_v, w_sem.at[1])
    wd_copy = pltpu.make_async_copy(wd_hbm.at[pl.ds(inner_at, inner)], wd_v, w_sem.at[2])
    wo_copy = pltpu.make_async_copy(wo_hbm.at[pl.ds(pl.multiple_of(corner * o_rows, o_rows), o_rows)], wo_v, w_sem.at[3])
    x_copy = pltpu.make_async_copy(x_hbm, x_v, x_sem.at[0])
    lnw_copy = pltpu.make_async_copy(lnw_hbm, lnw_v, x_sem.at[1])
    seq_copy = pltpu.make_async_copy(seq_hbm, seq_ref, x_sem.at[2])

    with jax.named_scope('entry'):
        barrier = pltpu.get_barrier_semaphore()

        def tell(to_tp, to_sp):
            pl.semaphore_signal(barrier, inc=1, device_id={'tp': to_tp, 'sp': to_sp}, device_id_type=MESH)

        x_copy.start()
        lnw_copy.start()
        tell(1 - tp, sp)
        for i in range(len(Q_CHUNKS)):
            wq_copy(i).start()
        seq_copy.start()
        for s in STEPS[:32]:
            tell(tp, step_to(s))
        k_copy(0).start()
        k_copy(1).start()
        for s in STEPS[32:]:
            tell(tp, step_to(s))
        for i in range(len(V_GROUPS)):
            v_copy(i).start()
        for f in FLIPS:
            tell(1 - tp, flip_to(f))
        wg_copy.start()
        wu_copy.start()

    with jax.named_scope('wait_x'):
        x_copy.wait()
    with jax.named_scope('wait_lnw'):
        lnw_copy.wait()
    with jax.named_scope('norm'):
        x_f32 = x_v[...].astype(jnp.float32)
        centered = x_f32 - jnp.mean(x_f32, axis=-1, keepdims=True)
        variance = jnp.mean(centered * centered, axis=-1, keepdims=True)
        scale = lnw_v[...].astype(jnp.float32).reshape(1, width)
        h_v[...] = (centered * lax.rsqrt(variance + LN_EPS) * scale).astype(jnp.bfloat16)

    with jax.named_scope('query'):
        query = jnp.zeros((n_rows, n_heads * head_dim), jnp.float32)
        for i in range(len(Q_CHUNKS)):
            wq_copy(i).wait()
            at = slice(q_starts[i], q_starts[i] + Q_CHUNKS[i])
            query += jnp.dot(h_v[:, at], wq_v[at, :], preferred_element_type=jnp.float32)
        query = query.astype(jnp.bfloat16).astype(jnp.float32)
        for h in range(n_heads):
            q_v[h * n_rows:(h + 1) * n_rows, :] = query[:, h * head_dim:(h + 1) * head_dim]

    low_lanes = lax.broadcasted_iota(jnp.int32, (1, head_dim), 1) < head_dim // 2
    first_kv = lax.broadcasted_iota(jnp.int32, (8, head_dim), 0) < 4
    positions = sp * seq_block + lax.broadcasted_iota(jnp.int32, (8, seq_block), 1)

    def score(b, j):
        at = pl.ds((b * per_row + j) * 8, 8)
        q8 = q_v[pl.ds(j * 8 * n_rows + b, 8, stride=n_rows), :]
        zero = jnp.zeros_like(q8)
        q_wide = jnp.concatenate([jnp.where(first_kv, q8, zero), jnp.where(first_kv, zero, q8)], axis=1)
        k_wide = jnp.concatenate([k_v[b, 2 * j], k_v[b, 2 * j + 1]], axis=1)
        s_v[at, :] = lax.dot_general(q_wide.astype(jnp.bfloat16), k_wide, (((1,), (1,)), ((), ())),
                                     preferred_element_type=jnp.float32)

    def soften(b, j):
        at = pl.ds((b * per_row + j) * 8, 8)
        is_live = positions <= seq_ref[b]
        scores = jnp.where(is_live, s_v[at, :] * head_dim ** -0.5, NEG_BIG)
        block_max = jnp.max(scores, axis=-1, keepdims=True)
        probs = jnp.where(is_live, jnp.exp(scores - block_max), 0.0)
        block_sum = jnp.sum(probs, axis=-1, keepdims=True)
        p_v[at, :] = probs
        any_live = block_sum > 0.0
        safe_sum = jnp.where(any_live, block_sum, 1.0)
        lse_v[at, :] = jnp.broadcast_to(jnp.where(any_live, block_max + jnp.log(safe_sum), NEG_BIG), (8, head_dim))
        stat_v[at, :] = jnp.broadcast_to(1.0 / safe_sum, (8, head_dim))

    def value(b, j):
        at = pl.ds((b * per_row + j) * 8, 8)
        v_wide = jnp.concatenate([v_v[b, 2 * j], v_v[b, 2 * j + 1]], axis=1)
        wide = jnp.dot(p_v[at, :].astype(jnp.bfloat16), v_wide, preferred_element_type=jnp.float32)
        o8 = jnp.where(first_kv, wide[:, :head_dim], wide[:, head_dim:]) * stat_v[at, :]
        lse8 = lse_v[at, :]
        for r in range(4):
            att_send[b * 8 + j * 4 + r, 0:2, :] = o8[2 * r:2 * r + 2]
            att_send[b * 8 + j * 4 + r, 2:3, :] = jnp.where(low_lanes, lse8[2 * r:2 * r + 1], lse8[2 * r + 1:2 * r + 2])

    def sets(start, n):
        return [(b, j) for b in range(start, start + n) for j in range(per_row)]

    with jax.named_scope('scores'):
        wd_copy.start()
        wo_copy.start()
        seq_copy.wait()
        k_copy(0).wait()
        for c in sets(0, n_rows // 2):
            score(*c)
        k_copy(1).wait()
        for c in sets(n_rows // 2, n_rows // 2):
            score(*c)
        for c in sets(0, n_rows // 2):
            soften(*c)
    with jax.named_scope('values'):
        for i in range(len(V_GROUPS)):
            v_copy(i).wait()
            if i == 0:
                for c in sets(n_rows // 2, n_rows // 2):
                    soften(*c)
            for c in sets(v_starts[i], V_GROUPS[i]):
                value(*c)

    with jax.named_scope('att_send'):
        pl.semaphore_wait(barrier, N_SP - 1 + N_CHIPS)
        for to, slot in in_order(COMBINE_ORDER):
            pltpu.make_async_remote_copy(
                src_ref=att_send.at[slot, pl.ds(0, 3)], dst_ref=att_recv.at[sp, pl.ds(0, 3)],
                send_sem=send_sem.at[0], recv_sem=att_rs,
                device_id={'tp': tp, 'sp': to}, device_id_type=MESH).start()
        att_recv[sp] = att_send[mine]

    with jax.named_scope('mlp'):
        wg_copy.wait()
        wu_copy.wait()
        wd_copy.wait()

        @pl.when(shares_mlp)
        def _():
            up_wide = jnp.concatenate([wg_v[...], wu_v[...]], axis=1)
            wide = jnp.dot(h_v[...], up_wide, preferred_element_type=jnp.float32)
            gate, up = wide[:, :inner], wide[:, inner:]
            act = (gate * jax.nn.sigmoid(gate) * up).astype(jnp.bfloat16)
            for c in range(N_CHIPS):
                part = jnp.dot(act, wd_v[:, c * piece:(c + 1) * piece], preferred_element_type=jnp.float32)
                for b in range(n_rows):
                    for r in range(piece_rows):
                        mlp_send[b * N_CHIPS + c, r:r + 1, :] = part[b:b + 1, r * LANES:(r + 1) * LANES]

    with jax.named_scope('mlp_send'):
        @pl.when(shares_mlp)
        def _():
            for to, slot in in_order(COMBINE_ORDER):
                pltpu.make_async_remote_copy(
                    src_ref=mlp_send.at[slot], dst_ref=mlp_recv.at[share], send_sem=send_sem.at[1], recv_sem=mlp_rs,
                    device_id={'tp': tp, 'sp': to}, device_id_type=MESH).start()
            mlp_recv[share] = mlp_send[mine]

        wo_copy.wait()

    others = att_recv.at[pl.ds(0, N_SP - 1), pl.ds(0, 3)]
    with jax.named_scope('att_wait'):
        pltpu.make_async_copy(others, others, att_rs).wait()
    with jax.named_scope('combine'):
        lse = att_recv[:, 2, :]
        weight = jnp.exp(lse - jnp.max(lse, axis=0, keepdims=True))
        swapped = pltpu.roll(weight, head_dim // 2, 1)
        attn = []
        for h in range(2):
            spread = jnp.where(low_lanes, weight, swapped) if h == 0 else jnp.where(low_lanes, swapped, weight)
            attn.append(jnp.sum(att_recv[:, h, :] * spread, axis=0, keepdims=True)
                        / jnp.sum(spread, axis=0, keepdims=True))
        attn = jnp.concatenate(attn, axis=1)
        is_row = lax.broadcasted_iota(jnp.int32, (n_rows, 2 * head_dim), 0) == row
        attn = jnp.where(is_row, jnp.broadcast_to(attn, is_row.shape), 0.0).astype(jnp.bfloat16)
        is_mine = lax.broadcasted_iota(jnp.int32, (n_rows, piece), 0) == row
    with jax.named_scope('out_proj'):
        member = corner * 2 + tp
        flips = FLIPS + [(0, 0, 0)]
        pieces_of = [4 * lax.rem(flip_z[f[0]], 2) + 2 * lax.rem(flip_y[f[1]], 2) + lax.rem(flip_x[f[2]], 2) for f in flips]
        for i in range(0, N_CHIPS, 4):
            for c in pieces_of[i:i + 4]:
                at = pl.ds(pl.multiple_of(c * piece, piece), piece)
                total = jnp.dot(attn, wo_v[:, at], preferred_element_type=jnp.float32)
                total = jnp.sum(jnp.where(is_mine, total, 0.0), axis=0, keepdims=True)
                for r in range(piece_rows):
                    sum_send[c, r:r + 1, :] = total[:, r * LANES:(r + 1) * LANES]
            for f, c in zip(flips[i:i + 4], pieces_of[i:i + 4]):
                for ptp in ((tp, 1 - tp) if any(f) else (1 - tp,)):
                    pltpu.make_async_remote_copy(
                        src_ref=sum_send.at[c], dst_ref=sum_recv.at[member], send_sem=send_sem.at[2], recv_sem=sum_rs,
                        device_id={'tp': ptp, 'sp': flip_to(f)}, device_id_type=MESH).start()
        sum_recv[member] = sum_send[corner]

    with jax.named_scope('mlp_wait'):
        for is_sender in (True, False):
            @pl.when(shares_mlp == is_sender)
            def _():
                heard = mlp_recv.at[pl.ds(0, N_INNER - is_sender)]
                pltpu.make_async_copy(heard, heard, mlp_rs).wait()

    with jax.named_scope('half_send'):
        half_send[...] = jnp.sum(mlp_recv[...], axis=0)
        half_copy = pltpu.make_async_remote_copy(
            src_ref=half_send, dst_ref=half_recv, send_sem=send_sem.at[2], recv_sem=half_rs,
            device_id={'tp': 1 - tp, 'sp': sp}, device_id_type=MESH)
        half_copy.start()
    pieces = sum_recv.at[pl.ds(0, N_GROUP - 1)]
    with jax.named_scope('sum_wait'):
        pltpu.make_async_copy(pieces, pieces, sum_rs).wait()
    with jax.named_scope('half_wait'):
        half_copy.wait_recv()

    with jax.named_scope('fin_send'):
        fin[mine] = jnp.sum(sum_recv[...], axis=0) + (half_send[...] + half_recv[...])
        for to, _ in in_order(FINISH_ORDER):
            pltpu.make_async_remote_copy(
                src_ref=fin.at[mine], dst_ref=fin.at[mine], send_sem=send_sem.at[3], recv_sem=fin_rs,
                device_id={'tp': tp, 'sp': to}, device_id_type=MESH).start()
    arrived = fin.at[pl.ds(0, N_SP - 1)]
    with jax.named_scope('fin_wait'):
        pltpu.make_async_copy(arrived, arrived, fin_rs).wait()
    with jax.named_scope('finish'):
        for c in range(width // LANES):
            m, r = c // piece_rows, c % piece_rows
            rows = jnp.concatenate([fin[b * N_CHIPS + m, r:r + 1, :] for b in range(n_rows)], axis=0)
            at = slice(c * LANES, (c + 1) * LANES)
            out_ref[:, at] = (x_v[:, at].astype(jnp.float32) + rows).astype(jnp.bfloat16)
    with jax.named_scope('drain'):
        pltpu.make_async_copy(others, others, send_sem.at[0]).wait()

        @pl.when(shares_mlp)
        def _():
            sent = mlp_send.at[pl.ds(0, N_SP - 1)]
            pltpu.make_async_copy(sent, sent, send_sem.at[1]).wait()

        both = fin.at[pl.ds(0, N_GROUP)]
        pltpu.make_async_copy(both, both, send_sem.at[2]).wait()
        pltpu.make_async_copy(arrived, arrived, send_sem.at[3]).wait()


def solution(mesh):
    cache_spec = P(None, 'tp', 'sp', None)
    col_spec = P(None, 'tp')
    row_spec = P('tp', None)

    def local_step(x, seq_len, ln_w, w_q, w_o, w_gate, w_up, w_down, k_cache, v_cache):
        n_rows, n_kv, seq_block, head_dim = k_cache.shape
        width = x.shape[1]
        q_width = w_q.shape[1]
        inner = w_gate.shape[1] // N_INNER
        piece_rows = width // N_CHIPS // LANES
        n_queries = n_rows * q_width // head_dim
        hbm = pl.BlockSpec(memory_space=pltpu.HBM)
        dma = pltpu.SemaphoreType.DMA
        return pl.pallas_call(
            kernel,
            out_shape=jax.ShapeDtypeStruct((n_rows, width), jnp.bfloat16),
            in_specs=[hbm] * 10,
            out_specs=pl.BlockSpec(memory_space=pltpu.VMEM),
            scratch_shapes=[
                pltpu.SMEM((n_rows,), jnp.int32),
                pltpu.VMEM((n_rows, width), jnp.bfloat16),
                pltpu.VMEM((width,), jnp.bfloat16),
                pltpu.VMEM((n_rows, width), jnp.bfloat16),
                pltpu.VMEM((width, q_width), jnp.bfloat16),
                pltpu.VMEM(k_cache.shape, jnp.bfloat16),
                pltpu.VMEM(v_cache.shape, jnp.bfloat16),
                pltpu.VMEM((width, inner), jnp.bfloat16),
                pltpu.VMEM((width, inner), jnp.bfloat16),
                pltpu.VMEM((inner, width), jnp.bfloat16),
                pltpu.VMEM((q_width // N_CHIPS, width), jnp.bfloat16),
                pltpu.VMEM((n_queries, head_dim), jnp.float32),
                pltpu.VMEM((n_queries, seq_block), jnp.float32),
                pltpu.VMEM((n_queries, seq_block), jnp.float32),
                pltpu.VMEM((n_queries, head_dim), jnp.float32),
                pltpu.VMEM((n_queries, head_dim), jnp.float32),
                pltpu.VMEM((N_SP, 4, LANES), jnp.float32),
                pltpu.VMEM((N_SP, 4, LANES), jnp.float32),
                pltpu.VMEM((N_SP, piece_rows, LANES), jnp.float32),
                pltpu.VMEM((N_INNER, piece_rows, LANES), jnp.float32),
                pltpu.VMEM((piece_rows, LANES), jnp.float32),
                pltpu.VMEM((piece_rows, LANES), jnp.float32),
                pltpu.VMEM((N_CHIPS, piece_rows, LANES), jnp.float32),
                pltpu.VMEM((N_GROUP, piece_rows, LANES), jnp.float32),
                pltpu.VMEM((N_SP, piece_rows, LANES), jnp.float32),
                dma((3,)), dma((len(Q_CHUNKS),)), dma((2,)), dma((len(V_GROUPS),)), dma((4,)),
                dma((4,)), dma, dma, dma, dma, dma,
            ],
            compiler_params=pltpu.CompilerParams(
                collective_id=0, has_side_effects=True, vmem_limit_bytes=40 * 1024 * 1024),
        )(*(pltpu.with_memory_space_constraint(a, pltpu.HBM)
            for a in (seq_len, x, ln_w, w_q, w_o, w_gate, w_up, w_down, k_cache, v_cache)))

    return jax.shard_map(local_step, mesh=mesh,
                         in_specs=(P(), P(), P(), col_spec, row_spec,
                                   col_spec, col_spec, row_spec, cache_spec, cache_spec),
                         out_specs=P(), check_vma=False)
```

profile of v0, /device:TPU:1, one launch (start us, length us, event | category | flops | bytes accessed | tf_op | source)
XLA Modules:
  0.0 29.7 jit_solution(15610815782068656200)
XLA Ops:
  0.0 29.1 %shard_map.100 = bf16[8,4096]{1,0:T(8,128)(2,1)S(1)} custom-call(s32[8]{0:T(128)} %seq_hbm.1, bf16[8,4096]{1,0:T(8,128)(2,1)} %x_hbm.1, bf16[4096]{0:T(1024)(128)(2,1)} %lnw_hbm.1, bf16[4096,2048]{1,0:T(8,128)(2,1)} %wq_hbm.1, bf16[2048,4096]{1,0:T(8,128)(2,1)} %wo_hbm.1, bf16[4096,6144]{1,0:T(8,128)(2,1)} %wg_hbm.1, bf16[4096,6144]{1,0:T(8,128)(2,1)} %wu_hbm.1, ...), custom_call_target="tpu_custom_call" | custom-call | tf_op jit(solution)/shard_map/pallas_call | solution.py:348
  29.1 0.6 %copy.12 = bf16[8,4096]{1,0:T(8,128)(2,1)} copy(bf16[8,4096]{1,0:T(8,128)(2,1)S(1)} %shard_map.100) | data formatting | bytes 131072
where the time goes:
time: 29.8 us; the launch traced here: 29.7 us
  Pallas kernels  29.1 us (98%)
  local copies, waits for them, and re-layouts  0.63 us (2%)
    pallas_call x1, Pallas kernels, local_step(): pl.pallas_call(kernel, out_shape=jax.ShapeDtypeStruct((n_rows, width), jn...  29.1 us
    unnamed x1, local copies, waits for them, and re-layouts  0.63 us

commit v1 on v0

--- a/solution.py
+++ b/solution.py
@@ -24,12 +24,7 @@
 
 STEPS = sorted(((dz, dy, dx) for dz in range(SIDE) for dy in range(SIDE) for dx in range(SIDE) if dz or dy or dx),
                key=lambda s: -sum(hops(d) for d in s))
-FINISH_ORDER = (
-    0, 12, 3, 1, 4, 16, 2, 57, 54, 8, 48, 35, 6, 19, 34, 36,
-    40, 7, 49, 42, 15, 56, 31, 25, 62, 37, 41, 14, 59, 28, 45, 11,
-    22, 32, 47, 58, 23, 44, 20, 60, 24, 51, 17, 46, 5, 43, 38, 9,
-    18, 52, 21, 53, 63, 29, 30, 26, 33, 61, 27, 10, 55, 39, 50, 13,
-)
+FINISH_STEPS = sorted(STEPS, key=lambda s: -sum((0.0, 1.37, 0.84, 0.42)[d] for d in s))
 FLIPS = sorted(((fz, fy, fx) for fz in range(2) for fy in range(2) for fx in range(2) if fz or fy or fx),
                key=lambda s: -sum(s))
 
@@ -305,10 +300,10 @@
 
     with jax.named_scope('fin_send'):
         fin[mine] = jnp.sum(sum_recv[...], axis=0) + (half_send[...] + half_recv[...])
-        for to, _ in in_order(FINISH_ORDER):
+        for s in FINISH_STEPS:
             pltpu.make_async_remote_copy(
                 src_ref=fin.at[mine], dst_ref=fin.at[mine], send_sem=send_sem.at[3], recv_sem=fin_rs,
-                device_id={'tp': tp, 'sp': to}, device_id_type=MESH).start()
+                device_id={'tp': tp, 'sp': step_to(s)}, device_id_type=MESH).start()
     arrived = fin.at[pl.ds(0, N_SP - 1)]
     with jax.named_scope('fin_wait'):
         pltpu.make_async_copy(arrived, arrived, fin_rs).wait()

time: 29.8 us -> 30.3 us (1.017)
  Pallas kernels: 29.1 us -> 29.6 us
    pallas_call x1, Pallas kernels: 29.1 us -> 29.6 us  [local_step(): pl.pallas_call(kernel, out_shape=jax.ShapeDtypeStruct((n_rows, width), jn...]
where the time goes in v1:
time: 30.3 us; the launch traced here: 30.2 us
  Pallas kernels  29.6 us (98%)
  local copies, waits for them, and re-layouts  0.63 us (2%)
    pallas_call x1, Pallas kernels, local_step(): pl.pallas_call(kernel, out_shape=jax.ShapeDtypeStruct((n_rows, width), jn...  29.6 us
    unnamed x1, local copies, waits for them, and re-layouts  0.63 us

profile of v1, /device:TPU:1, one launch (start us, length us, event | category | flops | bytes accessed | tf_op | source)
XLA Modules:
  0.0 30.2 jit_solution(8084362423979848800)
XLA Ops:
  0.0 29.6 %shard_map.100 = bf16[8,4096]{1,0:T(8,128)(2,1)S(1)} custom-call(s32[8]{0:T(128)} %seq_hbm.1, bf16[8,4096]{1,0:T(8,128)(2,1)} %x_hbm.1, bf16[4096]{0:T(1024)(128)(2,1)} %lnw_hbm.1, bf16[4096,2048]{1,0:T(8,128)(2,1)} %wq_hbm.1, bf16[2048,4096]{1,0:T(8,128)(2,1)} %wo_hbm.1, bf16[4096,6144]{1,0:T(8,128)(2,1)} %wg_hbm.1, bf16[4096,6144]{1,0:T(8,128)(2,1)} %wu_hbm.1, ...), custom_call_target="tpu_custom_call" | custom-call | tf_op jit(solution)/shard_map/pallas_call | solution.py:343
  29.6 0.6 %copy.12 = bf16[8,4096]{1,0:T(8,128)(2,1)} copy(bf16[8,4096]{1,0:T(8,128)(2,1)S(1)} %shard_map.100) | data formatting | bytes 131072
